TPU v7x, 32 devices: a whole 2x2x4 slice. The times are simulated.
32 devices in a mesh: gx: 4 (over y, core), gy: 2 (over x), gz: 4 (over z).
Axes of the slice: x: 2, y: 2, z: 4, core: 2. Of those that a mesh axis runs over, the one named last changes fastest.
Arguments:
- density: float32 [32, 32, 512], P('gx', 'gy', 'gz'), may hold values from 0.7 to 1.6
- momentum: float32 [32, 32, 512], P('gx', 'gy', 'gz'), may hold values from -7 to 7
- hydrogen: float32 [32, 32, 512], P('gx', 'gy', 'gz'), may hold values from 0.05 to 1.2
- forced_modes: int32 [96, 3], replicated, may hold values from -3 to 3, as said below
Outputs:
- density_rate: float32 [32, 32, 512], P('gx', 'gy', 'gz')
- momentum_rate: float32 [32, 32, 512], P('gx', 'gy', 'gz')
- hydrogen_rate: float32 [32, 32, 512], P('gx', 'gy', 'gz')
Inputs may be any that keep to these rules, and one draw needn't show every extreme that they name: `forced_modes`: each row is a wave vector (kx, ky, kz) with 1 <= kx^2 + ky^2 + kz^2 <= 9; the 96 rows are distinct.
All inputs are finite; a program needn't handle non-finite values.
Results may differ from a plain program's by a relative error of at most 0.0003.
Values sent between devices are 32-bit elements; how exact they have to be, the bound alone decides.
A program may use at most 64 MiB of HBM per device.

v0:
```python
import functools
import math

import jax
import jax.numpy as jnp
import numpy as np
from jax import lax
from jax.experimental import pallas as pl
from jax.experimental.pallas import tpu as pltpu
from jax.sharding import PartitionSpec as P

KMAX = 3
WIDTH = 2 * KMAX + 1
HALF = 64
ROWS = KMAX + 1
REACH = 4

FIRST_COEFFS = (0.8, -0.2, 4.0 / 105.0, -1.0 / 280.0)
SECOND_COEFFS = (1.6, -0.2, 8.0 / 315.0, -1.0 / 560.0)
CENTRE_COEFF = -205.0 / 72.0
VISCOSITY = 0.3
DIFFUSIVITY = 1.5
FORCE_POWER = 0.3
ENERGY_EPS = 1e-06
ACTIVATION = 2.0
HIGHEST = lax.Precision.HIGHEST
MESH = pl.DeviceIdType.MESH


def packed_modes():
    reach = range(-KMAX, KMAX + 1)
    cells = [(x, y, z) for z in range(ROWS) for x in reach for y in reach
             if x * x + y * y + z * z <= KMAX * KMAX and (z, x, y) > (0, 0, 0)]
    return cells


def packed_index(place):
    cells = packed_modes()
    result = []
    for part in range(3):
        value = jnp.full(place.shape, cells[0][part], jnp.int32)
        if part == 1:
            value = value + place
        for i in range(1, len(cells)):
            step = cells[i][part] - cells[i - 1][part] - (part == 1)
            if step:
                value = value + jnp.where(place >= i, step, 0)
        result.append(value)
    return result


def tables(local, full):
    size_x, size_y, size_z = local
    full_x, full_y, full_z = full
    k = np.arange(-KMAX, KMAX + 1)
    ang_z = 2.0 * np.pi * (k[:, None] * np.arange(size_z)[None, :]) / full_z
    trig_z = np.zeros((2 * ROWS, size_z))
    trig_z[:ROWS] = np.cos(ang_z[KMAX:])
    trig_z[ROWS:] = np.sin(ang_z[KMAX:])
    ax = k[:, None] * np.arange(size_x)[None, :] / full_x
    ay = k[:, None] * np.arange(size_y)[None, :] / full_y
    ang = np.stack([2.0 * np.pi * (ax[x + KMAX, :, None] + ay[y + KMAX, None, :]) for x, y, _ in packed_modes()])
    ang = ang.reshape(-1, size_x * size_y)
    trig_xy = np.zeros((2 * HALF, size_x * size_y))
    trig_xy[: len(ang)] = np.cos(ang)
    trig_xy[HALF : HALF + len(ang)] = np.sin(ang)
    edge = np.zeros((8, size_z))
    for j in range(REACH):
        edge[j, j] = 1.0
        edge[REACH + j, size_z - REACH + j] = 1.0
    band = np.zeros((size_z, size_z))
    halo = np.zeros((16, size_z))
    for z in range(size_z):
        band[z, z] = 3.0 * CENTRE_COEFF
        for offset, weight in enumerate(SECOND_COEFFS, 1):
            for q in (z - offset, z + offset):
                if 0 <= q < size_z:
                    band[q, z] = weight
                elif q < 0:
                    halo[8 + q, z] = weight
                else:
                    halo[8 + q - size_z, z] = weight
    z_high, z_low = split_host(trig_z)
    xy_high, xy_low = split_host(trig_xy)
    early = np.concatenate([z_high, z_low, xy_high, xy_low, z_high, z_high, z_low, z_low,
                            split_host(np.concatenate([edge, np.zeros_like(edge)], 0))[0]], 0)
    back = np.concatenate([xy_high, xy_low], 1)
    late = np.concatenate([halo, band], 0).astype(np.float32)
    return early, back, late


def split_host(table):
    high = table.astype(np.float32).astype(jnp.bfloat16)
    low = (table - high.astype(np.float64)).astype(np.float32).astype(jnp.bfloat16)
    return high, low


def split(x):
    high = x.astype(jnp.bfloat16).astype(jnp.float32)
    return high, x - high


def dot_split(a, b, contract):
    return lax.dot_general(a.astype(jnp.bfloat16), b.astype(jnp.bfloat16), (contract, ((), ())),
                           preferred_element_type=jnp.float32)


def fold(x):
    rows, lanes = x.shape
    x = x[: rows // 2] + x[rows // 2 :]
    return x[:, : lanes // 2] + x[:, lanes // 2 :]


def dot_nt(a, b):
    return lax.dot_general(a, b, (((1,), (1,)), ((), ())), precision=HIGHEST, preferred_element_type=jnp.float32)


def dot_nn(a, b):
    return lax.dot_general(a, b, (((1,), (0,)), ((), ())), precision=HIGHEST, preferred_element_type=jnp.float32)


def dot_tn(a, b):
    return lax.dot_general(a, b, (((0,), (0,)), ((), ())), precision=HIGHEST, preferred_element_type=jnp.float32)


def group_offsets(sizes, axes):
    offsets = [{}]
    for axis in axes:
        offsets = [{**o, axis: s} for o in offsets for s in range(sizes[axis])]
    return [o for o in offsets if any(o.values())]


def tree_sum(parts):
    parts = list(parts)
    while len(parts) > 1:
        parts = [sum(parts[i : i + 2][1:], parts[i]) for i in range(0, len(parts), 2)]
    return parts[0]


def plan(sizes):
    if math.prod(sizes.values()) <= 32:
        stages = [("gz", "gy", "gx")]
    elif sizes["gx"] * sizes["gy"] <= 16:
        stages = [("gz",), ("gx", "gy")]
    else:
        stages = [("gz",), ("gx",), ("gy",)]
    return [group_offsets(sizes, s)[::-1] for s in stages]


def kernel(sizes, local, dens_hbm, mom_hbm, fuel_hbm, modes_hbm, early_hbm, back_hbm, late_hbm,
           drate, mrate, hrate,
           f, modes, early, back, late, edges, sides, ypack, zpack, ztile, stage_own, stage_got,
           load_sem, halo_send, halo_recv, stage_send, stage_recv):
    size_x, size_y, size_z = local
    rows = size_x * size_y
    rows_z = 2 * ROWS
    me = {a: lax.axis_index(a) for a in sizes}
    stages = plan(sizes)

    def at(offset):
        return {a: lax.rem(me[a] + o, sizes[a]) for a, o in offset.items()}

    own = pl.ds(REACH, size_x)
    loads = [
        pltpu.make_async_copy(src, dst, load_sem.at[i])
        for i, (src, dst) in enumerate([
            (dens_hbm, f.at[0, own]), (mom_hbm, f.at[1, own]), (early_hbm, early),
            (fuel_hbm, f.at[2, own]), (modes_hbm, modes), (late_hbm, late), (back_hbm, back),
        ])
    ]
    for copy in loads:
        copy.start()
    barrier = pltpu.get_barrier_semaphore()
    partners = [o for group in stages for o in group]
    for offset in partners:
        pl.semaphore_signal(barrier, inc=1, device_id=at(offset), device_id_type=MESH)

    lane = lax.broadcasted_iota(jnp.int32, (1, 2 * HALF), 1)
    kx, ky, kz = packed_index(lax.rem(lane, HALF))
    turn = jnp.zeros((1, 2 * HALF), jnp.float32)
    for k, axis in ((kx, "gx"), (ky, "gy"), (kz, "gz")):
        part = k.astype(jnp.float32) * me[axis].astype(jnp.float32) / sizes[axis]
        turn = turn + (part - jnp.floor(part))
    level = (lax.broadcasted_iota(jnp.int32, (ROWS, 2 * HALF), 0) == kz).astype(jnp.float32)
    turn = turn - jnp.floor(turn + 0.5)
    cos_p = jnp.cos(2.0 * math.pi * turn)
    sin_p = jnp.sin(2.0 * math.pi * turn)
    sign = jnp.where(lane < HALF, -1.0, 1.0)
    sin_p = sign * sin_p

    loads[0].wait()
    loads[1].wait()
    loads[2].wait()
    flat = lambda i: f[i, own].reshape(rows, size_z)
    vel = flat(1) / flat(0)
    deep = 2 * rows_z
    table_xy = early[deep : deep + 4 * HALF]
    vel_both = jnp.concatenate(split(vel), 0)
    part = fold(dot_split(early[0:deep], vel_both, ((1,), (1,))))
    grid = fold(dot_split(jnp.concatenate(split(part), 0), table_xy, ((1,), (1,))))
    grid = grid * jnp.concatenate([level, level], 0)
    flip = jnp.sum(grid[ROWS:], axis=0, keepdims=True)
    cube = jnp.sum(grid[0:ROWS], axis=0, keepdims=True) + sign * pltpu.roll(flip, HALF, 1)
    cube = cos_p * cube + sin_p * pltpu.roll(cube, HALF, 1)
    stage_own[0] = cube

    def span(s):
        base = sum(len(g) for g in stages[:s])
        return pl.ds(base, len(stages[s]))

    def send_stage(s):
        base = sum(len(g) for g in stages[:s])
        for i, offset in enumerate(stages[s]):
            pltpu.make_async_remote_copy(
                src_ref=stage_own.at[s], dst_ref=stage_got.at[base + i],
                send_sem=stage_send.at[s], recv_sem=stage_recv.at[s],
                device_id=at(offset), device_id_type=MESH).start()

    def wait_stage(s, sem):
        got = stage_got.at[span(s)]
        pltpu.make_async_copy(got, got, sem.at[s]).wait()

    def sum_stage(s):
        base = sum(len(g) for g in stages[:s])
        wait_stage(s, stage_recv)
        return tree_sum([stage_own[s]] + [stage_got[base + i] for i in range(len(stages[s]))])

    loads[3].wait()
    pieces = []
    for i in range(2):
        ypack[i, :, 0:REACH] = f[1 + i, own, 0:REACH]
        ypack[i, :, REACH : 2 * REACH] = f[1 + i, own, size_y - REACH : size_y]
        high, rest = split(flat(1 + i))
        pieces += [high, *split(rest)]
    edge_at = deep + 4 * HALF + 4 * rows_z
    ends = dot_split(early[edge_at : edge_at + 16], jnp.concatenate(pieces, 0), ((1,), (1,)))[0:8]
    for i in range(2):
        zpack[i] = tree_sum([ends[:, (3 * i + j) * rows : (3 * i + j + 1) * rows] for j in range(3)])

    pl.semaphore_wait(barrier, len(partners))
    send_stage(0)

    def send(src, dst, slot, axis, step):
        copy = pltpu.make_async_remote_copy(
            src_ref=src, dst_ref=dst, send_sem=halo_send.at[slot // 2], recv_sem=halo_recv.at[slot // 2],
            device_id=at({axis: step % sizes[axis]}), device_id_type=MESH)
        copy.start()
        return copy

    halos_x = [
        send(f.at[:, pl.ds(size_x, REACH)], f.at[:, pl.ds(0, REACH)], 0, "gx", 1),
        send(f.at[:, pl.ds(REACH, REACH)], f.at[:, pl.ds(size_x + REACH, REACH)], 1, "gx", -1),
    ]
    halos_y = [send(ypack, sides.at[0], 2, "gy", 1)]
    if sizes["gy"] > 2:
        halos_y.append(send(ypack, sides.at[1], 3, "gy", -1))
    halos_z = [send(zpack, ztile.at[0], 4, "gz", 1), send(zpack, ztile.at[1], 5, "gz", -1)]

    loads[4].wait()
    count = modes.shape[1]
    code = (modes[0:1] * WIDTH + modes[1:2]) * WIDTH + modes[2:3]
    place = lax.rem(lax.broadcasted_iota(jnp.int32, (2 * HALF, 1), 0), HALF)
    px, py, pz = packed_index(place)
    mine = (px * WIDTH + py) * WIDTH + pz
    used = place < len(packed_modes())
    both_ways = jnp.where(used & (mine == code), 1.0, 0.0) + jnp.where(used & (mine == -code), 1.0, 0.0)
    chosen = dot_nt(jnp.ones((8, count), jnp.float32), both_ways)[0:1]

    loads[5].wait()
    lap = [dot_nn(flat(1 + i), late[16 : 16 + size_z]).reshape(size_x, size_y, size_z) for i in range(2)]
    outs = (drate, mrate, hrate)
    mrate[...] = lap[0]
    hrate[...] = lap[1]

    for s in range(1, len(stages)):
        stage_own[s] = sum_stage(s - 1)
        send_stage(s)

    arrived = [f.at[:, pl.ds(0, 2 * REACH)], sides.at[pl.ds(0, len(halos_y))], ztile]
    def wait_halo(sem, slot):
        pltpu.make_async_copy(arrived[slot], arrived[slot], sem.at[slot]).wait()

    wait_halo(halo_recv, 2)
    wait_halo(halo_recv, 1)
    for i in range(2):
        tile = jnp.concatenate([ztile[0, i], ztile[1, i]], 0)
        edges[i, :, 0:8] = sides[0, i]
        edges[i, :, 8 : 8 + size_y] = f[1 + i, own]
        edges[i, :, 8 + size_y : 16 + size_y] = sides[1 if sizes["gy"] > 2 else 0, i]
        total = outs[1 + i][...] + dot_tn(tile, late[0:16]).reshape(size_x, size_y, size_z)
        for offset, weight in enumerate(SECOND_COEFFS, 1):
            total = total + weight * (
                edges[i, :, 8 + offset : 8 + offset + size_y] + edges[i, :, 8 - offset : 8 - offset + size_y])
        outs[1 + i][...] = total

    wait_halo(halo_recv, 0)
    def planes(x, offset):
        return x[REACH + offset : REACH + offset + size_x]

    def first_diff(x):
        total = None
        for offset, weight in enumerate(FIRST_COEFFS, 1):
            term = weight * (planes(x, offset) - planes(x, -offset))
            total = term if total is None else total + term
        return total

    def second_diff(x):
        return tree_sum([w * (planes(x, o) + planes(x, -o)) for o, w in enumerate(SECOND_COEFFS, 1)])

    mom = f[1]
    dens = f[0]
    fuel = f[2]
    vel_pad = mom / dens
    drate[...] = -first_diff(mom)
    mid_fuel = planes(fuel, 0)
    hrate[...] = (DIFFUSIVITY * (hrate[...] + second_diff(fuel)) - first_diff(fuel * vel_pad)
                  - mid_fuel * jnp.exp(-ACTIVATION * mid_fuel / planes(dens, 0)))
    mrate[...] = VISCOSITY * (mrate[...] + second_diff(mom)) - first_diff(mom * vel_pad + dens)

    loads[6].wait()
    ncell = float(rows * size_z * math.prod(sizes.values()))
    cube = sum_stage(len(stages) - 1)
    coef = cube / ncell
    picked = chosen * coef
    energy = jnp.sum(jnp.sum(picked * coef, axis=1, keepdims=True), axis=0, keepdims=True)
    scale = 2.0 * FORCE_POWER / (energy + ENERGY_EPS)
    local_coef = cos_p * picked - sin_p * pltpu.roll(picked, HALF, 1)
    both = jnp.concatenate([level * local_coef, level * (-sign * pltpu.roll(local_coef, HALF, 1))], 0)
    wave = fold(dot_split(jnp.concatenate(split(both), 0), back[...], ((1,), (0,))))
    high, rest = split(wave)
    waves = jnp.concatenate([high, rest, high, rest], 0).T
    low = dot_split(waves, early[deep + 4 * HALF : deep + 4 * HALF + 4 * rows_z], ((1,), (0,)))
    low = low.reshape(size_x, size_y, size_z)
    mrate[...] = mrate[...] + f[0, own] * (low * scale.reshape(1, 1, 1))
    for slot in range(3):
        wait_halo(halo_send, slot)
    for s in range(len(stages)):
        wait_stage(s, stage_send)


def write_out(*refs):
    count = len(refs) // 2
    copies = [pltpu.make_async_copy(refs[i], refs[count + i], refs[-1].at[i]) for i in range(count)]
    for copy in copies:
        copy.start()
    for copy in copies:
        copy.wait()


def solution(mesh):
    sizes = {a: mesh.shape[a] for a in ("gx", "gy", "gz")}

    def per_device(density, momentum, hydrogen, forced_modes):
        local = density.shape
        size_x, size_y, size_z = local
        rows = size_x * size_y
        full = (size_x * sizes["gx"], size_y * sizes["gy"], size_z * sizes["gz"])
        early, back, late = tables(local, full)
        modes = forced_modes.T
        stages = plan(sizes)
        messages = sum(len(g) for g in stages)
        any_spec = pl.BlockSpec(memory_space=pl.ANY)
        f32 = jnp.float32
        rates = pl.pallas_call(
            functools.partial(kernel, sizes, local),
            out_shape=[pltpu.VMEM(local, f32)] * 3,
            in_specs=[any_spec] * 7,
            out_specs=[pl.BlockSpec(memory_space=pltpu.VMEM)] * 3,
            scratch_shapes=[
                pltpu.VMEM((3, size_x + 2 * REACH, size_y, size_z), f32),
                pltpu.VMEM(modes.shape, jnp.int32),
                pltpu.VMEM(early.shape, jnp.bfloat16),
                pltpu.VMEM(back.shape, jnp.bfloat16),
                pltpu.VMEM(late.shape, f32),
                pltpu.VMEM((2, size_x, size_y + 16, size_z), f32),
                pltpu.VMEM((2, 2, size_x, 8, size_z), f32),
                pltpu.VMEM((2, size_x, 8, size_z), f32),
                pltpu.VMEM((2, 8, rows), f32),
                pltpu.VMEM((2, 2, 8, rows), f32),
                pltpu.VMEM((len(stages), 1, 2 * HALF), f32),
                pltpu.VMEM((messages, 1, 2 * HALF), f32),
                pltpu.SemaphoreType.DMA((7,)),
                pltpu.SemaphoreType.DMA((3,)),
                pltpu.SemaphoreType.DMA((3,)),
                pltpu.SemaphoreType.DMA((len(stages),)),
                pltpu.SemaphoreType.DMA((len(stages),)),
            ],
            compiler_params=pltpu.CompilerParams(collective_id=0, has_side_effects=True),
            name="flame",
        )(density, momentum, hydrogen, modes, jnp.asarray(early), jnp.asarray(back), jnp.asarray(late))
        return tuple(pl.pallas_call(
            write_out,
            out_shape=[jax.ShapeDtypeStruct(local, f32)] * 3,
            in_specs=[pl.BlockSpec(memory_space=pltpu.VMEM)] * 3,
            out_specs=[any_spec] * 3,
            scratch_shapes=[pltpu.SemaphoreType.DMA((3,))],
            name="write",
        )(*[pltpu.with_memory_space_constraint(r, pltpu.VMEM) for r in rates]))

    in_specs = (P("gx", "gy", "gz"), P("gx", "gy", "gz"), P("gx", "gy", "gz"), P())
    out_specs = (P("gx", "gy", "gz"), P("gx", "gy", "gz"), P("gx", "gy", "gz"))
    return jax.shard_map(
        per_device, mesh=mesh, in_specs=in_specs, out_specs=out_specs, check_vma=False
    )
```

profile of v0, /device:TPU:0, one launch (start us, length us, event | category | flops | bytes accessed | tf_op | source)
XLA Modules:
  0.0 12.9 jit_solution(17999854035865758852)
XLA Ops:
  0.6 11.5 %flame.1 = (f32[8,16,128]{2,1,0:T(8,128)S(1)}, f32[8,16,128]{2,1,0:T(8,128)S(1)}, f32[8,16,128]{2,1,0:T(8,128)S(1)}) custom-call(f32[8,16,128]{2,1,0:T(8,128)} %dens_hbm.1, f32[8,16,128]{2,1,0:T(8,128)} %mom_hbm.1, f32[8,16,128]{2,1,0:T(8,128)} %fuel_hbm.1, s32[3,96]{1,0:T(4,128)} %bitcast.1, bf16[320,128]{1,0:T(8,128)(2,1)} %constant.6.clone.early_hbm, ...), custom_call_target="tpu_custom_call" | custom-call | tf_op jit(solution)/shard_map/flame/pallas_call | solution.py:364
  12.2 0.7 %write.1 = (f32[8,16,128]{2,1,0:T(8,128)}, f32[8,16,128]{2,1,0:T(8,128)}, f32[8,16,128]{2,1,0:T(8,128)}) custom-call(f32[8,16,128]{2,1,0:T(8,128)S(1)} %get-tuple-element.6.refs_0_, f32[8,16,128]{2,1,0:T(8,128)S(1)} %get-tuple-element.7.refs_1_, f32[8,16,128]{2,1,0:T(8,128)S(1)} %get-tuple-element.8.refs_2_), custom_call_target="tpu_custom_call" | custom-call | tf_op jit(solution)/shard_map/write/pallas_call | solution.py:391
where the time goes:
time: 13 us; the launch traced here: 12.9 us
  Pallas kernels  12.2 us (94%)
  between operations  0.64 us (5%)
    pallas_call x1, Pallas kernels, per_device(): pl.pallas_call(functools.partial(kernel, sizes, local), out_shape=[pltpu....  11.5 us
    pallas_call x1, Pallas kernels, per_device(): pl.pallas_call(write_out, out_shape=[jax.ShapeDtypeStruct(local, f32)] *...  0.7 us

commit v1 on v0

--- a/solution.py
+++ b/solution.py
@@ -123,13 +123,6 @@
     return lax.dot_general(a, b, (((0,), (0,)), ((), ())), precision=HIGHEST, preferred_element_type=jnp.float32)
 
 
-def group_offsets(sizes, axes):
-    offsets = [{}]
-    for axis in axes:
-        offsets = [{**o, axis: s} for o in offsets for s in range(sizes[axis])]
-    return [o for o in offsets if any(o.values())]
-
-
 def tree_sum(parts):
     parts = list(parts)
     while len(parts) > 1:
@@ -137,28 +130,32 @@
     return parts[0]
 
 
-def plan(sizes):
-    if math.prod(sizes.values()) <= 32:
-        stages = [("gz", "gy", "gx")]
-    elif sizes["gx"] * sizes["gy"] <= 16:
-        stages = [("gz",), ("gx", "gy")]
-    else:
-        stages = [("gz",), ("gx",), ("gy",)]
-    return [group_offsets(sizes, s)[::-1] for s in stages]
+def root_places(sizes):
+    return [{"gx": x, "gy": 0, "gz": 0} for x in range(min(2, sizes["gx"]))]
 
 
 def kernel(sizes, local, dens_hbm, mom_hbm, fuel_hbm, modes_hbm, early_hbm, back_hbm, late_hbm,
            drate, mrate, hrate,
-           f, modes, early, back, late, edges, sides, ypack, zpack, ztile, stage_own, stage_got,
-           load_sem, halo_send, halo_recv, stage_send, stage_recv):
+           f, modes, early, back, late, edges, sides, ypack, zpack, ztile, own_sum, got_sums, full_sum,
+           load_sem, halo_send, halo_recv, z_send, z_recv, sum_send, sum_recv, full_send, full_recv):
     size_x, size_y, size_z = local
     rows = size_x * size_y
     rows_z = 2 * ROWS
     me = {a: lax.axis_index(a) for a in sizes}
-    stages = plan(sizes)
-
-    def at(offset):
-        return {a: lax.rem(me[a] + o, sizes[a]) for a, o in offset.items()}
+    count_x, count_y, count_z = sizes["gx"], sizes["gy"], sizes["gz"]
+    total = count_x * count_y * count_z
+    roots = root_places(sizes)
+    rank_of = lambda p: (p["gz"] * count_x + p["gx"]) * count_y + p["gy"]
+    rank = rank_of(me)
+    root_ranks = [rank_of(r) for r in roots]
+    is_root = functools.reduce(jnp.logical_or, [rank == r for r in root_ranks])
+
+    def place_of(i):
+        return {"gx": lax.rem(lax.div(i, count_y), count_x), "gy": lax.rem(i, count_y),
+                "gz": lax.div(i, count_x * count_y)}
+
+    def shifted(axis, step):
+        return {axis: lax.rem(me[axis] + step % sizes[axis], sizes[axis])}
 
     own = pl.ds(REACH, size_x)
     loads = [
@@ -170,10 +167,38 @@
     ]
     for copy in loads:
         copy.start()
+
     barrier = pltpu.get_barrier_semaphore()
-    partners = [o for group in stages for o in group]
-    for offset in partners:
-        pl.semaphore_signal(barrier, inc=1, device_id=at(offset), device_id_type=MESH)
+    z_steps = (1, -1)
+    z_next = [shifted("gz", step)["gz"] for step in z_steps]
+    z_lower = [z < me["gz"] for z in z_next]
+    y_steps = (1, -1) if count_y > 2 else (1,)
+    sides_used = len(y_steps)
+
+    def greet(place):
+        pl.semaphore_signal(barrier, inc=1, device_id=place, device_id_type=MESH)
+
+    for step in (1, -1):
+        greet(shifted("gx", step))
+    for step in y_steps:
+        greet(shifted("gy", step))
+    for step, lower in zip(z_steps, z_lower):
+        @pl.when(jnp.logical_not(lower))
+        def _(step=step):
+            greet(shifted("gz", step))
+
+    @pl.when(is_root)
+    def _():
+        def greet_one(i, carry):
+            @pl.when(i != rank)
+            def _():
+                greet(place_of(i))
+            return carry
+        lax.fori_loop(0, total, greet_one, 0)
+
+    greeters = 2 + sides_used + len(roots) - is_root.astype(jnp.int32)
+    for lower in z_lower:
+        greeters = greeters + lower.astype(jnp.int32)
 
     lane = lax.broadcasted_iota(jnp.int32, (1, 2 * HALF), 1)
     kx, ky, kz = packed_index(lax.rem(lane, HALF))
@@ -202,30 +227,33 @@
     flip = jnp.sum(grid[ROWS:], axis=0, keepdims=True)
     cube = jnp.sum(grid[0:ROWS], axis=0, keepdims=True) + sign * pltpu.roll(flip, HALF, 1)
     cube = cos_p * cube + sin_p * pltpu.roll(cube, HALF, 1)
-    stage_own[0] = cube
-
-    def span(s):
-        base = sum(len(g) for g in stages[:s])
-        return pl.ds(base, len(stages[s]))
-
-    def send_stage(s):
-        base = sum(len(g) for g in stages[:s])
-        for i, offset in enumerate(stages[s]):
-            pltpu.make_async_remote_copy(
-                src_ref=stage_own.at[s], dst_ref=stage_got.at[base + i],
-                send_sem=stage_send.at[s], recv_sem=stage_recv.at[s],
-                device_id=at(offset), device_id_type=MESH).start()
-
-    def wait_stage(s, sem):
-        got = stage_got.at[span(s)]
-        pltpu.make_async_copy(got, got, sem.at[s]).wait()
-
-    def sum_stage(s):
-        base = sum(len(g) for g in stages[:s])
-        wait_stage(s, stage_recv)
-        return tree_sum([stage_own[s]] + [stage_got[base + i] for i in range(len(stages[s]))])
+    own_sum[...] = cube
+    got_sums[rank] = cube
+
+    pl.semaphore_wait(barrier, greeters)
+    to_root = [
+        pltpu.make_async_remote_copy(
+            src_ref=own_sum, dst_ref=got_sums.at[rank], send_sem=sum_send.at[i], recv_sem=sum_recv,
+            device_id={a: jnp.int32(v) for a, v in place.items()}, device_id_type=MESH)
+        for i, place in enumerate(roots)
+    ]
+    for copy, r in zip(to_root, root_ranks):
+        @pl.when(rank != r)
+        def _(copy=copy):
+            copy.start()
+
+    def send(src, dst, slot, axis, step):
+        copy = pltpu.make_async_remote_copy(
+            src_ref=src, dst_ref=dst, send_sem=halo_send.at[slot], recv_sem=halo_recv.at[slot],
+            device_id=shifted(axis, step), device_id_type=MESH)
+        copy.start()
+        return copy
 
     loads[3].wait()
+    halos_x = [
+        send(f.at[:, pl.ds(size_x, REACH)], f.at[:, pl.ds(0, REACH)], 0, "gx", 1),
+        send(f.at[:, pl.ds(REACH, REACH)], f.at[:, pl.ds(size_x + REACH, REACH)], 0, "gx", -1),
+    ]
     pieces = []
     for i in range(2):
         ypack[i, :, 0:REACH] = f[1 + i, own, 0:REACH]
@@ -236,25 +264,17 @@
     ends = dot_split(early[edge_at : edge_at + 16], jnp.concatenate(pieces, 0), ((1,), (1,)))[0:8]
     for i in range(2):
         zpack[i] = tree_sum([ends[:, (3 * i + j) * rows : (3 * i + j + 1) * rows] for j in range(3)])
-
-    pl.semaphore_wait(barrier, len(partners))
-    send_stage(0)
-
-    def send(src, dst, slot, axis, step):
-        copy = pltpu.make_async_remote_copy(
-            src_ref=src, dst_ref=dst, send_sem=halo_send.at[slot // 2], recv_sem=halo_recv.at[slot // 2],
-            device_id=at({axis: step % sizes[axis]}), device_id_type=MESH)
-        copy.start()
-        return copy
-
-    halos_x = [
-        send(f.at[:, pl.ds(size_x, REACH)], f.at[:, pl.ds(0, REACH)], 0, "gx", 1),
-        send(f.at[:, pl.ds(REACH, REACH)], f.at[:, pl.ds(size_x + REACH, REACH)], 1, "gx", -1),
+    halos_y = [send(ypack, sides.at[i], 1, "gy", step) for i, step in enumerate(y_steps)]
+    halos_z = [
+        pltpu.make_async_remote_copy(
+            src_ref=zpack, dst_ref=ztile.at[i], send_sem=z_send.at[i], recv_sem=z_recv.at[i],
+            device_id=shifted("gz", step), device_id_type=MESH)
+        for i, step in enumerate(z_steps)
     ]
-    halos_y = [send(ypack, sides.at[0], 2, "gy", 1)]
-    if sizes["gy"] > 2:
-        halos_y.append(send(ypack, sides.at[1], 3, "gy", -1))
-    halos_z = [send(zpack, ztile.at[0], 4, "gz", 1), send(zpack, ztile.at[1], 5, "gz", -1)]
+    for copy, lower in zip(halos_z, z_lower):
+        @pl.when(lower)
+        def _(copy=copy):
+            copy.start()
 
     loads[4].wait()
     count = modes.shape[1]
@@ -272,37 +292,31 @@
     mrate[...] = lap[0]
     hrate[...] = lap[1]
 
-    for s in range(1, len(stages)):
-        stage_own[s] = sum_stage(s - 1)
-        send_stage(s)
-
-    arrived = [f.at[:, pl.ds(0, 2 * REACH)], sides.at[pl.ds(0, len(halos_y))], ztile]
+    arrived = [f.at[:, pl.ds(0, 2 * REACH)], sides.at[pl.ds(0, sides_used)]]
     def wait_halo(sem, slot):
         pltpu.make_async_copy(arrived[slot], arrived[slot], sem.at[slot]).wait()
 
-    wait_halo(halo_recv, 2)
     wait_halo(halo_recv, 1)
     for i in range(2):
-        tile = jnp.concatenate([ztile[0, i], ztile[1, i]], 0)
         edges[i, :, 0:8] = sides[0, i]
         edges[i, :, 8 : 8 + size_y] = f[1 + i, own]
-        edges[i, :, 8 + size_y : 16 + size_y] = sides[1 if sizes["gy"] > 2 else 0, i]
-        total = outs[1 + i][...] + dot_tn(tile, late[0:16]).reshape(size_x, size_y, size_z)
+        edges[i, :, 8 + size_y : 16 + size_y] = sides[sides_used - 1, i]
+        total_y = outs[1 + i][...]
         for offset, weight in enumerate(SECOND_COEFFS, 1):
-            total = total + weight * (
+            total_y = total_y + weight * (
                 edges[i, :, 8 + offset : 8 + offset + size_y] + edges[i, :, 8 - offset : 8 - offset + size_y])
-        outs[1 + i][...] = total
+        outs[1 + i][...] = total_y
 
     wait_halo(halo_recv, 0)
     def planes(x, offset):
         return x[REACH + offset : REACH + offset + size_x]
 
     def first_diff(x):
-        total = None
+        result = None
         for offset, weight in enumerate(FIRST_COEFFS, 1):
             term = weight * (planes(x, offset) - planes(x, -offset))
-            total = term if total is None else total + term
-        return total
+            result = term if result is None else result + term
+        return result
 
     def second_diff(x):
         return tree_sum([w * (planes(x, o) + planes(x, -o)) for o, w in enumerate(SECOND_COEFFS, 1)])
@@ -317,9 +331,52 @@
                   - mid_fuel * jnp.exp(-ACTIVATION * mid_fuel / planes(dens, 0)))
     mrate[...] = VISCOSITY * (mrate[...] + second_diff(mom)) - first_diff(mom * vel_pad + dens)
 
+    from_next = [pltpu.make_async_copy(ztile.at[1 - i], ztile.at[1 - i], z_recv.at[1 - i]) for i in range(2)]
+    for copy, got, lower in zip(halos_z, from_next, z_lower):
+        @pl.when(jnp.logical_not(lower))
+        def _(copy=copy, got=got):
+            got.wait()
+            copy.start()
+    for got, lower in zip(from_next, z_lower):
+        @pl.when(lower)
+        def _(got=got):
+            got.wait()
+    for i, gain in enumerate((VISCOSITY, DIFFUSIVITY)):
+        tile = jnp.concatenate([ztile[0, i], ztile[1, i]], 0)
+        outs[1 + i][...] = outs[1 + i][...] + gain * dot_tn(tile, late[0:16]).reshape(size_x, size_y, size_z)
+
     loads[6].wait()
-    ncell = float(rows * size_z * math.prod(sizes.values()))
-    cube = sum_stage(len(stages) - 1)
+    def spread(i):
+        return pltpu.make_async_remote_copy(
+            src_ref=full_sum, dst_ref=full_sum, send_sem=full_send, recv_sem=full_recv,
+            device_id=place_of(i), device_id_type=MESH)
+
+    others = total - len(roots)
+
+    @pl.when(is_root)
+    def _():
+        got = got_sums.at[pl.ds(0, total - 1)]
+        pltpu.make_async_copy(got, got, sum_recv).wait()
+        full_sum[...] = tree_sum([got_sums[i] for i in range(total)])
+
+    if others:
+        @pl.when(rank == root_ranks[-1])
+        def _():
+            def send_one(j, carry):
+                i = total - 1 - j
+                leaf = functools.reduce(jnp.logical_and, [i != r for r in root_ranks])
+                @pl.when(leaf)
+                def _():
+                    spread(i).start()
+                return carry
+            lax.fori_loop(0, total, send_one, 0)
+
+        @pl.when(jnp.logical_not(is_root))
+        def _():
+            pltpu.make_async_copy(full_sum, full_sum, full_recv).wait()
+
+    ncell = float(rows * size_z * total)
+    cube = full_sum[...]
     coef = cube / ncell
     picked = chosen * coef
     energy = jnp.sum(jnp.sum(picked * coef, axis=1, keepdims=True), axis=0, keepdims=True)
@@ -332,10 +389,19 @@
     low = dot_split(waves, early[deep + 4 * HALF : deep + 4 * HALF + 4 * rows_z], ((1,), (0,)))
     low = low.reshape(size_x, size_y, size_z)
     mrate[...] = mrate[...] + f[0, own] * (low * scale.reshape(1, 1, 1))
-    for slot in range(3):
+    for slot in range(2):
         wait_halo(halo_send, slot)
-    for s in range(len(stages)):
-        wait_stage(s, stage_send)
+    for i in range(2):
+        pltpu.make_async_copy(zpack, zpack, z_send.at[i]).wait()
+    for i, r in enumerate(root_ranks):
+        @pl.when(rank != r)
+        def _(i=i):
+            pltpu.make_async_copy(own_sum, own_sum, sum_send.at[i]).wait()
+    if others:
+        @pl.when(rank == root_ranks[-1])
+        def _():
+            sent = got_sums.at[pl.ds(0, others)]
+            pltpu.make_async_copy(sent, sent, full_send).wait()
 
 
 def write_out(*refs):
@@ -357,8 +423,7 @@
         full = (size_x * sizes["gx"], size_y * sizes["gy"], size_z * sizes["gz"])
         early, back, late = tables(local, full)
         modes = forced_modes.T
-        stages = plan(sizes)
-        messages = sum(len(g) for g in stages)
+        total = math.prod(sizes.values())
         any_spec = pl.BlockSpec(memory_space=pl.ANY)
         f32 = jnp.float32
         rates = pl.pallas_call(
@@ -377,13 +442,18 @@
                 pltpu.VMEM((2, size_x, 8, size_z), f32),
                 pltpu.VMEM((2, 8, rows), f32),
                 pltpu.VMEM((2, 2, 8, rows), f32),
-                pltpu.VMEM((len(stages), 1, 2 * HALF), f32),
-                pltpu.VMEM((messages, 1, 2 * HALF), f32),
+                pltpu.VMEM((1, 2 * HALF), f32),
+                pltpu.VMEM((total, 1, 2 * HALF), f32),
+                pltpu.VMEM((1, 2 * HALF), f32),
                 pltpu.SemaphoreType.DMA((7,)),
-                pltpu.SemaphoreType.DMA((3,)),
-                pltpu.SemaphoreType.DMA((3,)),
-                pltpu.SemaphoreType.DMA((len(stages),)),
-                pltpu.SemaphoreType.DMA((len(stages),)),
+                pltpu.SemaphoreType.DMA((2,)),
+                pltpu.SemaphoreType.DMA((2,)),
+                pltpu.SemaphoreType.DMA((2,)),
+                pltpu.SemaphoreType.DMA((2,)),
+                pltpu.SemaphoreType.DMA((2,)),
+                pltpu.SemaphoreType.DMA,
+                pltpu.SemaphoreType.DMA,
+                pltpu.SemaphoreType.DMA,
             ],
             compiler_params=pltpu.CompilerParams(collective_id=0, has_side_effects=True),
             name="flame",

time: 13 us -> 12.4 us (0.954)
  the two profiles are of different devices: /device:TPU:0 before, /device:TPU:2 now
where the time goes in v1:
time: 12.4 us; the launch traced here: 12.2 us
  Pallas kernels  11.6 us (94%)
  between operations  0.64 us (5%)
    pallas_call x1, Pallas kernels, per_device(): pl.pallas_call(functools.partial(kernel, sizes, local), out_shape=[pltpu....  10.9 us
    pallas_call x1, Pallas kernels, per_device(): pl.pallas_call(write_out, out_shape=[jax.ShapeDtypeStruct(local, f32)] *...  0.7 us

profile of v1, /device:TPU:2, one launch (start us, length us, event | category | flops | bytes accessed | tf_op | source)
XLA Modules:
  0.0 12.2 jit_solution(4909431143953590849)
XLA Ops:
  0.6 10.9 %flame.1 = (f32[8,16,128]{2,1,0:T(8,128)S(1)}, f32[8,16,128]{2,1,0:T(8,128)S(1)}, f32[8,16,128]{2,1,0:T(8,128)S(1)}) custom-call(f32[8,16,128]{2,1,0:T(8,128)} %dens_hbm.1, f32[8,16,128]{2,1,0:T(8,128)} %mom_hbm.1, f32[8,16,128]{2,1,0:T(8,128)} %fuel_hbm.1, s32[3,96]{1,0:T(4,128)} %bitcast.1, bf16[320,128]{1,0:T(8,128)(2,1)} %constant.6.clone.early_hbm, ...), custom_call_target="tpu_custom_call" | custom-call | tf_op jit(solution)/shard_map/flame/pallas_call | solution.py:429
  11.5 0.7 %write.1 = (f32[8,16,128]{2,1,0:T(8,128)}, f32[8,16,128]{2,1,0:T(8,128)}, f32[8,16,128]{2,1,0:T(8,128)}) custom-call(f32[8,16,128]{2,1,0:T(8,128)S(1)} %get-tuple-element.6.refs_0_, f32[8,16,128]{2,1,0:T(8,128)S(1)} %get-tuple-element.7.refs_1_, f32[8,16,128]{2,1,0:T(8,128)S(1)} %get-tuple-element.8.refs_2_), custom_call_target="tpu_custom_call" | custom-call | tf_op jit(solution)/shard_map/write/pallas_call | solution.py:461

commit v2 on v1

--- a/solution.py
+++ b/solution.py
@@ -80,13 +80,9 @@
                     halo[8 + q, z] = weight
                 else:
                     halo[8 + q - size_z, z] = weight
-    z_high, z_low = split_host(trig_z)
-    xy_high, xy_low = split_host(trig_xy)
-    early = np.concatenate([z_high, z_low, xy_high, xy_low, z_high, z_high, z_low, z_low,
-                            split_host(np.concatenate([edge, np.zeros_like(edge)], 0))[0]], 0)
-    back = np.concatenate([xy_high, xy_low], 1)
-    late = np.concatenate([halo, band], 0).astype(np.float32)
-    return early, back, late
+    early = np.concatenate([*split_host(trig_z), *split_host(trig_xy)], 0)
+    late = np.concatenate([halo, band, trig_xy.T, edge, trig_z], 0).astype(np.float32)
+    return early, late
 
 
 def split_host(table):
@@ -109,6 +105,10 @@
     rows, lanes = x.shape
     x = x[: rows // 2] + x[rows // 2 :]
     return x[:, : lanes // 2] + x[:, lanes // 2 :]
+
+
+def sum_blocks(parts, rows):
+    return tree_sum([x[i : i + rows] for x in parts for i in range(0, x.shape[0], rows)])
 
 
 def dot_nt(a, b):
@@ -134,10 +134,10 @@
     return [{"gx": x, "gy": 0, "gz": 0} for x in range(min(2, sizes["gx"]))]
 
 
-def kernel(sizes, local, dens_hbm, mom_hbm, fuel_hbm, modes_hbm, early_hbm, back_hbm, late_hbm,
+def kernel(sizes, local, dens_hbm, mom_hbm, fuel_hbm, modes_hbm, early_hbm, late_hbm,
            drate, mrate, hrate,
-           f, modes, early, back, late, edges, sides, ypack, zpack, ztile, own_sum, got_sums, full_sum,
-           load_sem, halo_send, halo_recv, z_send, z_recv, sum_send, sum_recv, full_send, full_recv):
+           f, modes, early, late, turned, edges, sides, ypack, zpack, ztile, own_sum, got_sums, full_sum,
+           load_sem, send_sem, halo_recv, z_recv, sum_recv):
     size_x, size_y, size_z = local
     rows = size_x * size_y
     rows_z = 2 * ROWS
@@ -151,6 +151,9 @@
     is_root = functools.reduce(jnp.logical_or, [rank == r for r in root_ranks])
 
     def place_of(i):
+        if isinstance(i, int):
+            x, y, z = i // count_y % count_x, i % count_y, i // (count_x * count_y)
+            return {"gx": jnp.int32(x), "gy": jnp.int32(y), "gz": jnp.int32(z)}
         return {"gx": lax.rem(lax.div(i, count_y), count_x), "gy": lax.rem(i, count_y),
                 "gz": lax.div(i, count_x * count_y)}
 
@@ -158,15 +161,15 @@
         return {axis: lax.rem(me[axis] + step % sizes[axis], sizes[axis])}
 
     own = pl.ds(REACH, size_x)
-    loads = [
-        pltpu.make_async_copy(src, dst, load_sem.at[i])
-        for i, (src, dst) in enumerate([
-            (dens_hbm, f.at[0, own]), (mom_hbm, f.at[1, own]), (early_hbm, early),
-            (fuel_hbm, f.at[2, own]), (modes_hbm, modes), (late_hbm, late), (back_hbm, back),
-        ])
-    ]
-    for copy in loads:
-        copy.start()
+    load_early = pltpu.make_async_copy(early_hbm, early, load_sem.at[1])
+    load_late = pltpu.make_async_copy(late_hbm, late, load_sem.at[1])
+    load_dens = pltpu.make_async_copy(dens_hbm, f.at[0, own], load_sem.at[0])
+    load_mom = pltpu.make_async_copy(mom_hbm, f.at[1, own], load_sem.at[0])
+    load_fuel = pltpu.make_async_copy(fuel_hbm, f.at[2, own], load_sem.at[0])
+    load_modes = pltpu.make_async_copy(modes_hbm, modes, load_sem.at[0])
+    load_dens.start()
+    load_mom.start()
+    load_early.start()
 
     barrier = pltpu.get_barrier_semaphore()
     z_steps = (1, -1)
@@ -206,77 +209,86 @@
     for k, axis in ((kx, "gx"), (ky, "gy"), (kz, "gz")):
         part = k.astype(jnp.float32) * me[axis].astype(jnp.float32) / sizes[axis]
         turn = turn + (part - jnp.floor(part))
-    level = (lax.broadcasted_iota(jnp.int32, (ROWS, 2 * HALF), 0) == kz).astype(jnp.float32)
     turn = turn - jnp.floor(turn + 0.5)
     cos_p = jnp.cos(2.0 * math.pi * turn)
     sin_p = jnp.sin(2.0 * math.pi * turn)
     sign = jnp.where(lane < HALF, -1.0, 1.0)
-    sin_p = sign * sin_p
-
-    loads[0].wait()
-    loads[1].wait()
-    loads[2].wait()
+    row = lax.broadcasted_iota(jnp.int32, (rows_z, 2 * HALF), 0)
+    first = (row == kz).astype(jnp.float32)
+    second = (row == kz + ROWS).astype(jnp.float32)
+    turn_own = first * cos_p - second * sin_p
+    turn_swap = first * (sign * sin_p) + second * (sign * cos_p)
+
+    both_loaded = f.at[pl.ds(0, 2), own]
+    pltpu.make_async_copy(both_loaded, both_loaded, load_sem.at[0]).wait()
+    load_early.wait()
+    load_fuel.start()
+    load_late.start()
     flat = lambda i: f[i, own].reshape(rows, size_z)
     vel = flat(1) / flat(0)
     deep = 2 * rows_z
-    table_xy = early[deep : deep + 4 * HALF]
-    vel_both = jnp.concatenate(split(vel), 0)
-    part = fold(dot_split(early[0:deep], vel_both, ((1,), (1,))))
-    grid = fold(dot_split(jnp.concatenate(split(part), 0), table_xy, ((1,), (1,))))
-    grid = grid * jnp.concatenate([level, level], 0)
-    flip = jnp.sum(grid[ROWS:], axis=0, keepdims=True)
-    cube = jnp.sum(grid[0:ROWS], axis=0, keepdims=True) + sign * pltpu.roll(flip, HALF, 1)
-    cube = cos_p * cube + sin_p * pltpu.roll(cube, HALF, 1)
+    part = sum_blocks([dot_split(early[0:deep], x, ((1,), (1,))) for x in split(vel)], rows_z)
+    part_both = jnp.concatenate(split(part), 0)
+    cells = [early[deep + i * HALF : deep + (i + 1) * HALF] for i in range(4)]
+    grid, swap = [
+        fold(dot_split(part_both, jnp.concatenate([cells[i] for i in order], 0), ((1,), (1,))))
+        for order in ((0, 1, 2, 3), (1, 0, 3, 2))
+    ]
+    cube = jnp.sum(turn_own * grid + turn_swap * swap, axis=0, keepdims=True)
     own_sum[...] = cube
     got_sums[rank] = cube
 
     pl.semaphore_wait(barrier, greeters)
-    to_root = [
-        pltpu.make_async_remote_copy(
-            src_ref=own_sum, dst_ref=got_sums.at[rank], send_sem=sum_send.at[i], recv_sem=sum_recv,
-            device_id={a: jnp.int32(v) for a, v in place.items()}, device_id_type=MESH)
-        for i, place in enumerate(roots)
+    def copy_out(src, dst, recv, place):
+        return pltpu.make_async_remote_copy(
+            src_ref=src, dst_ref=dst, send_sem=send_sem, recv_sem=recv, device_id=place, device_id_type=MESH)
+
+    def spread(i):
+        return copy_out(full_sum, full_sum, sum_recv, place_of(i))
+
+    for r in root_ranks:
+        @pl.when(rank != r)
+        def _(r=r):
+            copy_out(own_sum, got_sums.at[rank], sum_recv, place_of(r)).start()
+
+    load_fuel.wait()
+    load_modes.start()
+    halos_x = [
+        copy_out(f.at[:, pl.ds(size_x, REACH)], f.at[:, pl.ds(0, REACH)], halo_recv.at[0], shifted("gx", 1)),
+        copy_out(f.at[:, pl.ds(REACH, REACH)], f.at[:, pl.ds(size_x + REACH, REACH)], halo_recv.at[0],
+                 shifted("gx", -1)),
     ]
-    for copy, r in zip(to_root, root_ranks):
-        @pl.when(rank != r)
-        def _(copy=copy):
-            copy.start()
-
-    def send(src, dst, slot, axis, step):
-        copy = pltpu.make_async_remote_copy(
-            src_ref=src, dst_ref=dst, send_sem=halo_send.at[slot], recv_sem=halo_recv.at[slot],
-            device_id=shifted(axis, step), device_id_type=MESH)
+    for copy in halos_x:
         copy.start()
-        return copy
-
-    loads[3].wait()
-    halos_x = [
-        send(f.at[:, pl.ds(size_x, REACH)], f.at[:, pl.ds(0, REACH)], 0, "gx", 1),
-        send(f.at[:, pl.ds(REACH, REACH)], f.at[:, pl.ds(size_x + REACH, REACH)], 0, "gx", -1),
-    ]
+    load_late.wait()
+    band_at = 16
+    trig_at = band_at + size_z
+    edge_at = trig_at + rows
+    wave_at = edge_at + 8
     pieces = []
     for i in range(2):
         ypack[i, :, 0:REACH] = f[1 + i, own, 0:REACH]
         ypack[i, :, REACH : 2 * REACH] = f[1 + i, own, size_y - REACH : size_y]
         high, rest = split(flat(1 + i))
         pieces += [high, *split(rest)]
-    edge_at = deep + 4 * HALF + 4 * rows_z
-    ends = dot_split(early[edge_at : edge_at + 16], jnp.concatenate(pieces, 0), ((1,), (1,)))[0:8]
+    ends = dot_split(late[edge_at : edge_at + 8], jnp.concatenate(pieces, 0), ((1,), (1,)))
     for i in range(2):
         zpack[i] = tree_sum([ends[:, (3 * i + j) * rows : (3 * i + j + 1) * rows] for j in range(3)])
-    halos_y = [send(ypack, sides.at[i], 1, "gy", step) for i, step in enumerate(y_steps)]
-    halos_z = [
-        pltpu.make_async_remote_copy(
-            src_ref=zpack, dst_ref=ztile.at[i], send_sem=z_send.at[i], recv_sem=z_recv.at[i],
-            device_id=shifted("gz", step), device_id_type=MESH)
-        for i, step in enumerate(z_steps)
-    ]
+    halos_y = [copy_out(ypack, sides.at[i], halo_recv.at[1], shifted("gy", step)) for i, step in enumerate(y_steps)]
+    halos_z = [copy_out(zpack, ztile.at[i], z_recv.at[i], shifted("gz", step)) for i, step in enumerate(z_steps)]
     for copy, lower in zip(halos_z, z_lower):
         @pl.when(lower)
         def _(copy=copy):
             copy.start()
-
-    loads[4].wait()
+    for copy in halos_y:
+        copy.start()
+
+    lap = [dot_nn(flat(1 + i), late[band_at : band_at + size_z]).reshape(size_x, size_y, size_z) for i in range(2)]
+    outs = (drate, mrate, hrate)
+    mrate[...] = lap[0]
+    hrate[...] = lap[1]
+
+    load_modes.wait()
     count = modes.shape[1]
     code = (modes[0:1] * WIDTH + modes[1:2]) * WIDTH + modes[2:3]
     place = lax.rem(lax.broadcasted_iota(jnp.int32, (2 * HALF, 1), 0), HALF)
@@ -286,17 +298,23 @@
     both_ways = jnp.where(used & (mine == code), 1.0, 0.0) + jnp.where(used & (mine == -code), 1.0, 0.0)
     chosen = dot_nt(jnp.ones((8, count), jnp.float32), both_ways)[0:1]
 
-    loads[5].wait()
-    lap = [dot_nn(flat(1 + i), late[16 : 16 + size_z]).reshape(size_x, size_y, size_z) for i in range(2)]
-    outs = (drate, mrate, hrate)
-    mrate[...] = lap[0]
-    hrate[...] = lap[1]
+    ncell = float(rows * size_z * total)
+    gain = chosen * (2.0 * FORCE_POWER / ncell)
+    cells_xy = late[trig_at : trig_at + rows]
+    cells_swap = pltpu.roll(cells_xy, HALF, 1)
+    signed = sign * sin_p
+    for i, table in enumerate((
+            (gain * cos_p) * cells_xy + (gain * signed) * cells_swap,
+            (gain * sign * cos_p) * cells_swap - (gain * sign * signed) * cells_xy)):
+        high, rest = split(table)
+        turned[:, 2 * HALF * i : 2 * HALF * (i + 1)] = high.astype(jnp.bfloat16)
+        turned[:, 2 * HALF * (2 + i) : 2 * HALF * (3 + i)] = rest.astype(jnp.bfloat16)
 
     arrived = [f.at[:, pl.ds(0, 2 * REACH)], sides.at[pl.ds(0, sides_used)]]
-    def wait_halo(sem, slot):
-        pltpu.make_async_copy(arrived[slot], arrived[slot], sem.at[slot]).wait()
-
-    wait_halo(halo_recv, 1)
+    def wait_halo(slot):
+        pltpu.make_async_copy(arrived[slot], arrived[slot], halo_recv.at[slot]).wait()
+
+    wait_halo(1)
     for i in range(2):
         edges[i, :, 0:8] = sides[0, i]
         edges[i, :, 8 : 8 + size_y] = f[1 + i, own]
@@ -307,7 +325,7 @@
                 edges[i, :, 8 + offset : 8 + offset + size_y] + edges[i, :, 8 - offset : 8 - offset + size_y])
         outs[1 + i][...] = total_y
 
-    wait_halo(halo_recv, 0)
+    wait_halo(0)
     def planes(x, offset):
         return x[REACH + offset : REACH + offset + size_x]
 
@@ -341,17 +359,11 @@
         @pl.when(lower)
         def _(got=got):
             got.wait()
-    for i, gain in enumerate((VISCOSITY, DIFFUSIVITY)):
+    for i, rate in enumerate((VISCOSITY, DIFFUSIVITY)):
         tile = jnp.concatenate([ztile[0, i], ztile[1, i]], 0)
-        outs[1 + i][...] = outs[1 + i][...] + gain * dot_tn(tile, late[0:16]).reshape(size_x, size_y, size_z)
-
-    loads[6].wait()
-    def spread(i):
-        return pltpu.make_async_remote_copy(
-            src_ref=full_sum, dst_ref=full_sum, send_sem=full_send, recv_sem=full_recv,
-            device_id=place_of(i), device_id_type=MESH)
-
-    others = total - len(roots)
+        outs[1 + i][...] = outs[1 + i][...] + rate * dot_tn(tile, late[0:16]).reshape(size_x, size_y, size_z)
+
+    leaves = [i for i in range(total) if i not in root_ranks]
 
     @pl.when(is_root)
     def _():
@@ -359,54 +371,51 @@
         pltpu.make_async_copy(got, got, sum_recv).wait()
         full_sum[...] = tree_sum([got_sums[i] for i in range(total)])
 
-    if others:
+    if leaves:
         @pl.when(rank == root_ranks[-1])
         def _():
-            def send_one(j, carry):
-                i = total - 1 - j
-                leaf = functools.reduce(jnp.logical_and, [i != r for r in root_ranks])
-                @pl.when(leaf)
-                def _():
-                    spread(i).start()
-                return carry
-            lax.fori_loop(0, total, send_one, 0)
+            for i in reversed(leaves):
+                spread(i).start()
 
         @pl.when(jnp.logical_not(is_root))
         def _():
-            pltpu.make_async_copy(full_sum, full_sum, full_recv).wait()
-
-    ncell = float(rows * size_z * total)
+            pltpu.make_async_copy(full_sum, full_sum, sum_recv).wait()
+
     cube = full_sum[...]
     coef = cube / ncell
-    picked = chosen * coef
-    energy = jnp.sum(jnp.sum(picked * coef, axis=1, keepdims=True), axis=0, keepdims=True)
-    scale = 2.0 * FORCE_POWER / (energy + ENERGY_EPS)
-    local_coef = cos_p * picked - sin_p * pltpu.roll(picked, HALF, 1)
-    both = jnp.concatenate([level * local_coef, level * (-sign * pltpu.roll(local_coef, HALF, 1))], 0)
-    wave = fold(dot_split(jnp.concatenate(split(both), 0), back[...], ((1,), (0,))))
-    high, rest = split(wave)
-    waves = jnp.concatenate([high, rest, high, rest], 0).T
-    low = dot_split(waves, early[deep + 4 * HALF : deep + 4 * HALF + 4 * rows_z], ((1,), (0,)))
-    low = low.reshape(size_x, size_y, size_z)
-    mrate[...] = mrate[...] + f[0, own] * (low * scale.reshape(1, 1, 1))
-    for slot in range(2):
-        wait_halo(halo_send, slot)
-    for i in range(2):
-        pltpu.make_async_copy(zpack, zpack, z_send.at[i]).wait()
-    for i, r in enumerate(root_ranks):
+    energy = jnp.sum(chosen * coef * coef, axis=1, keepdims=True)
+    scale = 1.0 / (energy + ENERGY_EPS)
+    split_cube = split(jnp.concatenate([first * cube, second * cube], 1))
+    high, rest = [jnp.concatenate([x] * 4, 0).astype(jnp.bfloat16) for x in split_cube]
+    right = jnp.concatenate([high, high, rest], 1)
+    wave_high, wave_rest = split(late[wave_at : wave_at + rows_z])
+    right_z = jnp.concatenate([wave_high, wave_high, wave_rest, wave_rest], 0)
+    use_rest = lax.rem(lax.broadcasted_iota(jnp.int32, (rows // 2, 4 * rows_z), 1), 2 * rows_z) >= rows_z
+    for half in range(2):
+        here = pl.ds(half * rows // 2, rows // 2)
+        left = jnp.concatenate([turned[here], turned[here, 0 : 4 * HALF]], 1)
+        high, rest = split(dot_split(left, right, ((1,), (1,))))
+        low = dot_split(jnp.where(use_rest, rest, high), right_z, ((1,), (0,)))
+        low = low.reshape(size_x // 2, size_y, size_z)
+        at = pl.ds(half * size_x // 2, size_x // 2)
+        mrate[at] = mrate[at] + f[0, pl.ds(REACH + half * size_x // 2, size_x // 2)] * (low * scale.reshape(1, 1, 1))
+
+    for sent in (arrived[0], arrived[1], ztile.at[:, :]):
+        pltpu.make_async_copy(sent, sent, send_sem).wait()
+    for r in root_ranks:
         @pl.when(rank != r)
-        def _(i=i):
-            pltpu.make_async_copy(own_sum, own_sum, sum_send.at[i]).wait()
-    if others:
+        def _():
+            pltpu.make_async_copy(own_sum, own_sum, send_sem).wait()
+    if leaves:
         @pl.when(rank == root_ranks[-1])
         def _():
-            sent = got_sums.at[pl.ds(0, others)]
-            pltpu.make_async_copy(sent, sent, full_send).wait()
+            sent = got_sums.at[pl.ds(0, len(leaves))]
+            pltpu.make_async_copy(sent, sent, send_sem).wait()
 
 
 def write_out(*refs):
     count = len(refs) // 2
-    copies = [pltpu.make_async_copy(refs[i], refs[count + i], refs[-1].at[i]) for i in range(count)]
+    copies = [pltpu.make_async_copy(refs[i], refs[count + i], refs[-1]) for i in range(count)]
     for copy in copies:
         copy.start()
     for copy in copies:
@@ -421,7 +430,7 @@
         size_x, size_y, size_z = local
         rows = size_x * size_y
         full = (size_x * sizes["gx"], size_y * sizes["gy"], size_z * sizes["gz"])
-        early, back, late = tables(local, full)
+        early, late = tables(local, full)
         modes = forced_modes.T
         total = math.prod(sizes.values())
         any_spec = pl.BlockSpec(memory_space=pl.ANY)
@@ -429,14 +438,14 @@
         rates = pl.pallas_call(
             functools.partial(kernel, sizes, local),
             out_shape=[pltpu.VMEM(local, f32)] * 3,
-            in_specs=[any_spec] * 7,
+            in_specs=[any_spec] * 6,
             out_specs=[pl.BlockSpec(memory_space=pltpu.VMEM)] * 3,
             scratch_shapes=[
                 pltpu.VMEM((3, size_x + 2 * REACH, size_y, size_z), f32),
                 pltpu.VMEM(modes.shape, jnp.int32),
                 pltpu.VMEM(early.shape, jnp.bfloat16),
-                pltpu.VMEM(back.shape, jnp.bfloat16),
                 pltpu.VMEM(late.shape, f32),
+                pltpu.VMEM((rows, 8 * HALF), jnp.bfloat16),
                 pltpu.VMEM((2, size_x, size_y + 16, size_z), f32),
                 pltpu.VMEM((2, 2, size_x, 8, size_z), f32),
                 pltpu.VMEM((2, size_x, 8, size_z), f32),
@@ -445,25 +454,21 @@
                 pltpu.VMEM((1, 2 * HALF), f32),
                 pltpu.VMEM((total, 1, 2 * HALF), f32),
                 pltpu.VMEM((1, 2 * HALF), f32),
-                pltpu.SemaphoreType.DMA((7,)),
+                pltpu.SemaphoreType.DMA((2,)),
+                pltpu.SemaphoreType.DMA,
                 pltpu.SemaphoreType.DMA((2,)),
                 pltpu.SemaphoreType.DMA((2,)),
-                pltpu.SemaphoreType.DMA((2,)),
-                pltpu.SemaphoreType.DMA((2,)),
-                pltpu.SemaphoreType.DMA((2,)),
-                pltpu.SemaphoreType.DMA,
-                pltpu.SemaphoreType.DMA,
                 pltpu.SemaphoreType.DMA,
             ],
             compiler_params=pltpu.CompilerParams(collective_id=0, has_side_effects=True),
             name="flame",
-        )(density, momentum, hydrogen, modes, jnp.asarray(early), jnp.asarray(back), jnp.asarray(late))
+        )(density, momentum, hydrogen, modes, jnp.asarray(early), jnp.asarray(late))
         return tuple(pl.pallas_call(
             write_out,
             out_shape=[jax.ShapeDtypeStruct(local, f32)] * 3,
             in_specs=[pl.BlockSpec(memory_space=pltpu.VMEM)] * 3,
             out_specs=[any_spec] * 3,
-            scratch_shapes=[pltpu.SemaphoreType.DMA((3,))],
+            scratch_shapes=[pltpu.SemaphoreType.DMA],
             name="write",
         )(*[pltpu.with_memory_space_constraint(r, pltpu.VMEM) for r in rates]))
 

time: 12.4 us -> 11.8 us (0.952)
  the two profiles are of different devices: /device:TPU:2 before, /device:TPU:0 now
where the time goes in v2:
time: 11.8 us; the launch traced here: 11.7 us
  Pallas kernels  11 us (93%)
  between operations  0.64 us (5%)
    pallas_call x1, Pallas kernels, per_device(): pl.pallas_call(functools.partial(kernel, sizes, local), out_shape=[pltpu....  10.3 us
    pallas_call x1, Pallas kernels, per_device(): pl.pallas_call(write_out, out_shape=[jax.ShapeDtypeStruct(local, f32)] *...  0.68 us

profile of v2, /device:TPU:0, one launch (start us, length us, event | category | flops | bytes accessed | tf_op | source)
XLA Modules:
  0.0 11.7 jit_solution(5008117590782534227)
XLA Ops:
  0.6 10.3 %flame.1 = (f32[8,16,128]{2,1,0:T(8,128)S(1)}, f32[8,16,128]{2,1,0:T(8,128)S(1)}, f32[8,16,128]{2,1,0:T(8,128)S(1)}) custom-call(f32[8,16,128]{2,1,0:T(8,128)} %dens_hbm.1, f32[8,16,128]{2,1,0:T(8,128)} %mom_hbm.1, f32[8,16,128]{2,1,0:T(8,128)} %fuel_hbm.1, s32[3,96]{1,0:T(4,128)} %bitcast.1, bf16[272,128]{1,0:T(8,128)(2,1)} %constant.4.clone.early_hbm, ...), custom_call_target="tpu_custom_call" | custom-call | tf_op jit(solution)/shard_map/flame/pallas_call | solution.py:438
  11.0 0.7 %write.1 = (f32[8,16,128]{2,1,0:T(8,128)}, f32[8,16,128]{2,1,0:T(8,128)}, f32[8,16,128]{2,1,0:T(8,128)}) custom-call(f32[8,16,128]{2,1,0:T(8,128)S(1)} %get-tuple-element.6.refs_0_, f32[8,16,128]{2,1,0:T(8,128)S(1)} %get-tuple-element.7.refs_1_, f32[8,16,128]{2,1,0:T(8,128)S(1)} %get-tuple-element.8.refs_2_), custom_call_target="tpu_custom_call" | custom-call | tf_op jit(solution)/shard_map/write/pallas_call | solution.py:466

commit v3 on v2

--- a/solution.py
+++ b/solution.py
@@ -14,6 +14,7 @@
 HALF = 64
 ROWS = KMAX + 1
 REACH = 4
+LOAD_PLANES = 4
 
 FIRST_COEFFS = (0.8, -0.2, 4.0 / 105.0, -1.0 / 280.0)
 SECOND_COEFFS = (1.6, -0.2, 8.0 / 315.0, -1.0 / 560.0)
@@ -49,21 +50,7 @@
     return result
 
 
-def tables(local, full):
-    size_x, size_y, size_z = local
-    full_x, full_y, full_z = full
-    k = np.arange(-KMAX, KMAX + 1)
-    ang_z = 2.0 * np.pi * (k[:, None] * np.arange(size_z)[None, :]) / full_z
-    trig_z = np.zeros((2 * ROWS, size_z))
-    trig_z[:ROWS] = np.cos(ang_z[KMAX:])
-    trig_z[ROWS:] = np.sin(ang_z[KMAX:])
-    ax = k[:, None] * np.arange(size_x)[None, :] / full_x
-    ay = k[:, None] * np.arange(size_y)[None, :] / full_y
-    ang = np.stack([2.0 * np.pi * (ax[x + KMAX, :, None] + ay[y + KMAX, None, :]) for x, y, _ in packed_modes()])
-    ang = ang.reshape(-1, size_x * size_y)
-    trig_xy = np.zeros((2 * HALF, size_x * size_y))
-    trig_xy[: len(ang)] = np.cos(ang)
-    trig_xy[HALF : HALF + len(ang)] = np.sin(ang)
+def tables(size_z):
     edge = np.zeros((8, size_z))
     for j in range(REACH):
         edge[j, j] = 1.0
@@ -80,15 +67,33 @@
                     halo[8 + q, z] = weight
                 else:
                     halo[8 + q - size_z, z] = weight
-    early = np.concatenate([*split_host(trig_z), *split_host(trig_xy)], 0)
-    late = np.concatenate([halo, band, trig_xy.T, edge, trig_z], 0).astype(np.float32)
-    return early, late
-
-
-def split_host(table):
-    high = table.astype(np.float32).astype(jnp.bfloat16)
-    low = (table - high.astype(np.float64)).astype(np.float32).astype(jnp.bfloat16)
-    return high, low
+    return np.concatenate([halo, band, edge], 0).astype(np.float32)
+
+
+def polynomial(x, coeffs):
+    result = coeffs[-1]
+    for c in reversed(coeffs[:-1]):
+        result = result * x + c
+    return result
+
+
+SIN_COEFFS = [(-1) ** n * (math.pi / 2) ** (2 * n + 1) / math.factorial(2 * n + 1) for n in range(5)]
+COS_COEFFS = [(-1) ** n * (math.pi / 2) ** (2 * n) / math.factorial(2 * n) for n in range(6)]
+
+
+def cos_sin(quarters):
+    turns = jnp.floor(quarters + 0.5)
+    d = quarters - turns
+    square = d * d
+    s = d * polynomial(square, SIN_COEFFS)
+    c = polynomial(square, COS_COEFFS)
+    half = jnp.floor(0.5 * turns)
+    odd = turns - 2.0 * half
+    turned = half - 2.0 * jnp.floor(0.5 * half)
+    sin_sign = 1.0 - 2.0 * turned
+    cos_sign = sin_sign - 2.0 * odd * sin_sign
+    swap = odd > 0.5
+    return jnp.where(swap, s, c) * cos_sign, jnp.where(swap, c, s) * sin_sign
 
 
 def split(x):
@@ -101,14 +106,9 @@
                            preferred_element_type=jnp.float32)
 
 
-def fold(x):
-    rows, lanes = x.shape
-    x = x[: rows // 2] + x[rows // 2 :]
-    return x[:, : lanes // 2] + x[:, lanes // 2 :]
-
-
-def sum_blocks(parts, rows):
-    return tree_sum([x[i : i + rows] for x in parts for i in range(0, x.shape[0], rows)])
+def column_sum(x):
+    x = tree_sum([x[i : i + 8] for i in range(0, x.shape[0], 8)])
+    return jnp.sum(x, axis=0, keepdims=True)
 
 
 def dot_nt(a, b):
@@ -134,13 +134,12 @@
     return [{"gx": x, "gy": 0, "gz": 0} for x in range(min(2, sizes["gx"]))]
 
 
-def kernel(sizes, local, dens_hbm, mom_hbm, fuel_hbm, modes_hbm, early_hbm, late_hbm,
+def kernel(sizes, local, dens_hbm, mom_hbm, fuel_hbm, modes_hbm, late_hbm,
            drate, mrate, hrate,
-           f, modes, early, late, turned, edges, sides, ypack, zpack, ztile, own_sum, got_sums, full_sum,
-           load_sem, send_sem, halo_recv, z_recv, sum_recv):
+           f, modes, late, cells, along, along_low, across, across_low, edges, sides, ypack, zpack, ztile, own_sum, got_sums, full_sum,
+           load_sem, send_sem, halo_recv, z_recv, sum_recv, z_ready):
     size_x, size_y, size_z = local
     rows = size_x * size_y
-    rows_z = 2 * ROWS
     me = {a: lax.axis_index(a) for a in sizes}
     count_x, count_y, count_z = sizes["gx"], sizes["gy"], sizes["gz"]
     total = count_x * count_y * count_z
@@ -161,15 +160,13 @@
         return {axis: lax.rem(me[axis] + step % sizes[axis], sizes[axis])}
 
     own = pl.ds(REACH, size_x)
-    load_early = pltpu.make_async_copy(early_hbm, early, load_sem.at[1])
     load_late = pltpu.make_async_copy(late_hbm, late, load_sem.at[1])
-    load_dens = pltpu.make_async_copy(dens_hbm, f.at[0, own], load_sem.at[0])
-    load_mom = pltpu.make_async_copy(mom_hbm, f.at[1, own], load_sem.at[0])
+    for at in range(0, size_x, LOAD_PLANES):
+        for i, src in enumerate((dens_hbm, mom_hbm)):
+            pltpu.make_async_copy(
+                src.at[pl.ds(at, LOAD_PLANES)], f.at[i, pl.ds(REACH + at, LOAD_PLANES)], load_sem.at[0]).start()
     load_fuel = pltpu.make_async_copy(fuel_hbm, f.at[2, own], load_sem.at[0])
     load_modes = pltpu.make_async_copy(modes_hbm, modes, load_sem.at[0])
-    load_dens.start()
-    load_mom.start()
-    load_early.start()
 
     barrier = pltpu.get_barrier_semaphore()
     z_steps = (1, -1)
@@ -205,36 +202,36 @@
 
     lane = lax.broadcasted_iota(jnp.int32, (1, 2 * HALF), 1)
     kx, ky, kz = packed_index(lax.rem(lane, HALF))
-    turn = jnp.zeros((1, 2 * HALF), jnp.float32)
-    for k, axis in ((kx, "gx"), (ky, "gy"), (kz, "gz")):
-        part = k.astype(jnp.float32) * me[axis].astype(jnp.float32) / sizes[axis]
-        turn = turn + (part - jnp.floor(part))
-    turn = turn - jnp.floor(turn + 0.5)
-    cos_p = jnp.cos(2.0 * math.pi * turn)
-    sin_p = jnp.sin(2.0 * math.pi * turn)
-    sign = jnp.where(lane < HALF, -1.0, 1.0)
-    row = lax.broadcasted_iota(jnp.int32, (rows_z, 2 * HALF), 0)
-    first = (row == kz).astype(jnp.float32)
-    second = (row == kz + ROWS).astype(jnp.float32)
-    turn_own = first * cos_p - second * sin_p
-    turn_swap = first * (sign * sin_p) + second * (sign * cos_p)
+    quarter = (lane >= HALF).astype(jnp.float32)
+    kx, ky, kz = [k.astype(jnp.float32) for k in (kx, ky, kz)]
+
+    def quarters(k, place, axis, size):
+        part = k * place.astype(jnp.float32) / (size * sizes[axis])
+        return 4.0 * (part - jnp.floor(part))
+
+    shift = quarters(kz, me["gz"] * size_z, "gz", size_z) - quarter
+    rows_y = me["gy"] * size_y + lax.broadcasted_iota(jnp.int32, (size_y, 1), 0)
+    angle_y = quarters(ky, rows_y, "gy", size_y) + shift
+    for x in range(size_x):
+        c, s = cos_sin(angle_y + quarters(kx, me["gx"] * size_x + x, "gx", size_x))
+        cells[x * size_y : (x + 1) * size_y, 0 : 2 * HALF] = c
+        cells[x * size_y : (x + 1) * size_y, 2 * HALF : 4 * HALF] = -s
+    for z in range(0, size_z, 16):
+        rows_at = z + lax.broadcasted_iota(jnp.int32, (16, 1), 0)
+        for i, x in enumerate(cos_sin(quarters(kz, rows_at, "gz", size_z))):
+            high, rest = split(x)
+            along[z : z + 16, 2 * HALF * i : 2 * HALF * (i + 1)] = high.astype(jnp.bfloat16)
+            along_low[z : z + 16, 2 * HALF * i : 2 * HALF * (i + 1)] = rest.astype(jnp.bfloat16)
 
     both_loaded = f.at[pl.ds(0, 2), own]
     pltpu.make_async_copy(both_loaded, both_loaded, load_sem.at[0]).wait()
-    load_early.wait()
     load_fuel.start()
     load_late.start()
     flat = lambda i: f[i, own].reshape(rows, size_z)
-    vel = flat(1) / flat(0)
-    deep = 2 * rows_z
-    part = sum_blocks([dot_split(early[0:deep], x, ((1,), (1,))) for x in split(vel)], rows_z)
-    part_both = jnp.concatenate(split(part), 0)
-    cells = [early[deep + i * HALF : deep + (i + 1) * HALF] for i in range(4)]
-    grid, swap = [
-        fold(dot_split(part_both, jnp.concatenate([cells[i] for i in order], 0), ((1,), (1,))))
-        for order in ((0, 1, 2, 3), (1, 0, 3, 2))
-    ]
-    cube = jnp.sum(turn_own * grid + turn_swap * swap, axis=0, keepdims=True)
+    high, rest = split(flat(1) / flat(0))
+    part = (dot_split(jnp.concatenate([high, rest], 1), jnp.concatenate([along[...], along[...]], 0), ((1,), (0,)))
+            + dot_split(high, along_low[...], ((1,), (0,)))) * cells[...]
+    cube = column_sum(part[:, 0 : 2 * HALF] + part[:, 2 * HALF : 4 * HALF])
     own_sum[...] = cube
     got_sums[rank] = cube
 
@@ -250,6 +247,11 @@
         @pl.when(rank != r)
         def _(r=r):
             copy_out(own_sum, got_sums.at[rank], sum_recv, place_of(r)).start()
+
+    for step, lower in zip(z_steps, z_lower):
+        @pl.when(lower)
+        def _(step=step):
+            pl.semaphore_signal(z_ready, inc=1, device_id=shifted("gz", step), device_id_type=MESH)
 
     load_fuel.wait()
     load_modes.start()
@@ -262,9 +264,7 @@
         copy.start()
     load_late.wait()
     band_at = 16
-    trig_at = band_at + size_z
-    edge_at = trig_at + rows
-    wave_at = edge_at + 8
+    edge_at = band_at + size_z
     pieces = []
     for i in range(2):
         ypack[i, :, 0:REACH] = f[1 + i, own, 0:REACH]
@@ -300,19 +300,25 @@
 
     ncell = float(rows * size_z * total)
     gain = chosen * (2.0 * FORCE_POWER / ncell)
-    cells_xy = late[trig_at : trig_at + rows]
-    cells_swap = pltpu.roll(cells_xy, HALF, 1)
-    signed = sign * sin_p
-    for i, table in enumerate((
-            (gain * cos_p) * cells_xy + (gain * signed) * cells_swap,
-            (gain * sign * cos_p) * cells_swap - (gain * sign * signed) * cells_xy)):
-        high, rest = split(table)
-        turned[:, 2 * HALF * i : 2 * HALF * (i + 1)] = high.astype(jnp.bfloat16)
-        turned[:, 2 * HALF * (2 + i) : 2 * HALF * (3 + i)] = rest.astype(jnp.bfloat16)
+    for i in range(2):
+        here = pl.ds(2 * HALF * i, 2 * HALF)
+        across[here] = along[:, here].astype(jnp.float32).T.astype(jnp.bfloat16)
+        across_low[here] = along_low[:, here].astype(jnp.float32).T.astype(jnp.bfloat16)
 
     arrived = [f.at[:, pl.ds(0, 2 * REACH)], sides.at[pl.ds(0, sides_used)]]
     def wait_halo(slot):
         pltpu.make_async_copy(arrived[slot], arrived[slot], halo_recv.at[slot]).wait()
+
+    higher = sum(jnp.logical_not(lower).astype(jnp.int32) for lower in z_lower)
+
+    @pl.when(higher > 0)
+    def _():
+        pl.semaphore_wait(z_ready, higher)
+
+    for copy, lower in zip(halos_z, z_lower):
+        @pl.when(jnp.logical_not(lower))
+        def _(copy=copy):
+            copy.start()
 
     wait_halo(1)
     for i in range(2):
@@ -349,16 +355,8 @@
                   - mid_fuel * jnp.exp(-ACTIVATION * mid_fuel / planes(dens, 0)))
     mrate[...] = VISCOSITY * (mrate[...] + second_diff(mom)) - first_diff(mom * vel_pad + dens)
 
-    from_next = [pltpu.make_async_copy(ztile.at[1 - i], ztile.at[1 - i], z_recv.at[1 - i]) for i in range(2)]
-    for copy, got, lower in zip(halos_z, from_next, z_lower):
-        @pl.when(jnp.logical_not(lower))
-        def _(copy=copy, got=got):
-            got.wait()
-            copy.start()
-    for got, lower in zip(from_next, z_lower):
-        @pl.when(lower)
-        def _(got=got):
-            got.wait()
+    for i in range(2):
+        pltpu.make_async_copy(ztile.at[i], ztile.at[i], z_recv.at[i]).wait()
     for i, rate in enumerate((VISCOSITY, DIFFUSIVITY)):
         tile = jnp.concatenate([ztile[0, i], ztile[1, i]], 0)
         outs[1 + i][...] = outs[1 + i][...] + rate * dot_tn(tile, late[0:16]).reshape(size_x, size_y, size_z)
@@ -385,20 +383,12 @@
     coef = cube / ncell
     energy = jnp.sum(chosen * coef * coef, axis=1, keepdims=True)
     scale = 1.0 / (energy + ENERGY_EPS)
-    split_cube = split(jnp.concatenate([first * cube, second * cube], 1))
-    high, rest = [jnp.concatenate([x] * 4, 0).astype(jnp.bfloat16) for x in split_cube]
-    right = jnp.concatenate([high, high, rest], 1)
-    wave_high, wave_rest = split(late[wave_at : wave_at + rows_z])
-    right_z = jnp.concatenate([wave_high, wave_high, wave_rest, wave_rest], 0)
-    use_rest = lax.rem(lax.broadcasted_iota(jnp.int32, (rows // 2, 4 * rows_z), 1), 2 * rows_z) >= rows_z
-    for half in range(2):
-        here = pl.ds(half * rows // 2, rows // 2)
-        left = jnp.concatenate([turned[here], turned[here, 0 : 4 * HALF]], 1)
-        high, rest = split(dot_split(left, right, ((1,), (1,))))
-        low = dot_split(jnp.where(use_rest, rest, high), right_z, ((1,), (0,)))
-        low = low.reshape(size_x // 2, size_y, size_z)
-        at = pl.ds(half * size_x // 2, size_x // 2)
-        mrate[at] = mrate[at] + f[0, pl.ds(REACH + half * size_x // 2, size_x // 2)] * (low * scale.reshape(1, 1, 1))
+    lit = gain * cube
+    high, rest = split(cells[...] * jnp.concatenate([lit, lit], 1))
+    both = dot_split(high, jnp.concatenate([across[...], across_low[...]], 1), ((1,), (0,)))
+    low = both[:, 0:size_z] + both[:, size_z:] + dot_split(rest, across[...], ((1,), (0,)))
+    low = low.reshape(size_x, size_y, size_z)
+    mrate[...] = mrate[...] + f[0, own] * (low * scale.reshape(1, 1, 1))
 
     for sent in (arrived[0], arrived[1], ztile.at[:, :]):
         pltpu.make_async_copy(sent, sent, send_sem).wait()
@@ -429,8 +419,7 @@
         local = density.shape
         size_x, size_y, size_z = local
         rows = size_x * size_y
-        full = (size_x * sizes["gx"], size_y * sizes["gy"], size_z * sizes["gz"])
-        early, late = tables(local, full)
+        late = tables(size_z)
         modes = forced_modes.T
         total = math.prod(sizes.values())
         any_spec = pl.BlockSpec(memory_space=pl.ANY)
@@ -438,14 +427,17 @@
         rates = pl.pallas_call(
             functools.partial(kernel, sizes, local),
             out_shape=[pltpu.VMEM(local, f32)] * 3,
-            in_specs=[any_spec] * 6,
+            in_specs=[any_spec] * 5,
             out_specs=[pl.BlockSpec(memory_space=pltpu.VMEM)] * 3,
             scratch_shapes=[
                 pltpu.VMEM((3, size_x + 2 * REACH, size_y, size_z), f32),
                 pltpu.VMEM(modes.shape, jnp.int32),
-                pltpu.VMEM(early.shape, jnp.bfloat16),
                 pltpu.VMEM(late.shape, f32),
-                pltpu.VMEM((rows, 8 * HALF), jnp.bfloat16),
+                pltpu.VMEM((rows, 4 * HALF), f32),
+                pltpu.VMEM((size_z, 4 * HALF), jnp.bfloat16),
+                pltpu.VMEM((size_z, 4 * HALF), jnp.bfloat16),
+                pltpu.VMEM((4 * HALF, size_z), jnp.bfloat16),
+                pltpu.VMEM((4 * HALF, size_z), jnp.bfloat16),
                 pltpu.VMEM((2, size_x, size_y + 16, size_z), f32),
                 pltpu.VMEM((2, 2, size_x, 8, size_z), f32),
                 pltpu.VMEM((2, size_x, 8, size_z), f32),
@@ -459,10 +451,11 @@
                 pltpu.SemaphoreType.DMA((2,)),
                 pltpu.SemaphoreType.DMA((2,)),
                 pltpu.SemaphoreType.DMA,
+                pltpu.SemaphoreType.REGULAR,
             ],
             compiler_params=pltpu.CompilerParams(collective_id=0, has_side_effects=True),
             name="flame",
-        )(density, momentum, hydrogen, modes, jnp.asarray(early), jnp.asarray(late))
+        )(density, momentum, hydrogen, modes, jnp.asarray(late))
         return tuple(pl.pallas_call(
             write_out,
             out_shape=[jax.ShapeDtypeStruct(local, f32)] * 3,

time: 11.8 us -> 11.4 us (0.966)
  Pallas kernels: 11 us -> 10.5 us
    pallas_call x1, Pallas kernels: 10.3 us -> 9.84 us  [per_device(): pl.pallas_call(functools.partial(kernel, sizes, local), out_shape=[pltpu....]
where the time goes in v3:
time: 11.4 us; the launch traced here: 11.2 us
  Pallas kernels  10.5 us (92%)
  between operations  0.64 us (6%)
    pallas_call x1, Pallas kernels, per_device(): pl.pallas_call(functools.partial(kernel, sizes, local), out_shape=[pltpu....  9.84 us
    pallas_call x1, Pallas kernels, per_device(): pl.pallas_call(write_out, out_shape=[jax.ShapeDtypeStruct(local, f32)] *...  0.68 us

profile of v3, /device:TPU:0, one launch (start us, length us, event | category | flops | bytes accessed | tf_op | source)
XLA Modules:
  0.0 11.2 jit_solution(4778371872587419235)
XLA Ops:
  0.6 9.8 %flame.1 = (f32[8,16,128]{2,1,0:T(8,128)S(1)}, f32[8,16,128]{2,1,0:T(8,128)S(1)}, f32[8,16,128]{2,1,0:T(8,128)S(1)}) custom-call(f32[8,16,128]{2,1,0:T(8,128)} %dens_hbm.1, f32[8,16,128]{2,1,0:T(8,128)} %mom_hbm.1, f32[8,16,128]{2,1,0:T(8,128)} %fuel_hbm.1, s32[3,96]{1,0:T(4,128)} %bitcast.1, f32[152,128]{1,0:T(8,128)} %constant.2.clone.late_hbm), custom_call_target="tpu_custom_call" | custom-call | tf_op jit(solution)/shard_map/flame/pallas_call | solution.py:427
  10.5 0.7 %write.1 = (f32[8,16,128]{2,1,0:T(8,128)}, f32[8,16,128]{2,1,0:T(8,128)}, f32[8,16,128]{2,1,0:T(8,128)}) custom-call(f32[8,16,128]{2,1,0:T(8,128)S(1)} %get-tuple-element.6.refs_0_, f32[8,16,128]{2,1,0:T(8,128)S(1)} %get-tuple-element.7.refs_1_, f32[8,16,128]{2,1,0:T(8,128)S(1)} %get-tuple-element.8.refs_2_), custom_call_target="tpu_custom_call" | custom-call | tf_op jit(solution)/shard_map/write/pallas_call | solution.py:459
